TPU v7x, 16 devices: a 4x2x1 block of a 4x4x8 slice. The times are simulated.
16 devices in a mesh: data: 2 (over y, z), model: 8 (over x, core).
Axes of the slice: x: 4, y: 2, z: 1, core: 2. Of those that a mesh axis runs over, the one named last changes fastest.
The devices are a block of a 4x4x8 slice.
Arguments:
- queries: bfloat16 [512, 1024], P('data'), parts along dimension 0
- w_head: bfloat16 [1024, 50304], P(None, 'model')
- ds_keys: bfloat16 [524288, 1024], P('model')
- ds_tokens: int32 [524288], P('model')
- temperature: float32 [1], replicated
- mix_weight: float32 [1], replicated
Outputs:
- output: float32 [512, 50304], P('data', 'model'), parts along dimension 0
There are 2 independent parts. A program takes and returns all parts, laid end to end along the dimension named above; an argument that names none is the same for every part.
All inputs are finite; a program needn't handle non-finite values.
Results may differ from a plain program's by a relative error of at most 0.001.
Values are sent between devices in bfloat16 or wider.
A program may use at most 768 MiB of HBM per device.

v0:
```python
import jax
import jax.numpy as jnp
from jax import lax
from jax.sharding import PartitionSpec as P


def solution(mesh):
    group_size = mesh.shape["model"]

    def local_step(queries, w_shard, key_shard, tok_shard, value_a11, mix_weight):
        row_count = queries.shape[0]
        vocab_size = w_shard.shape[1] * group_size
        cross_dot = jnp.einsum("bd,nd->bn", queries, key_shard, preferred_element_type=jnp.float32)
        key_sq = jnp.sum(jnp.square(key_shard.astype(jnp.float32)), axis=1)
        scores = (2.0 * cross_dot - key_sq[None, :]) / value_a11[0]
        row_max = lax.pmax(jnp.max(scores, axis=1), "model")
        weights = jnp.exp(scores - row_max[:, None])
        row_total = lax.psum(jnp.sum(weights, axis=1), "model")
        local_hist = jnp.zeros((row_count, vocab_size), jnp.float32).at[:, tok_shard].add(weights)
        histogram = lax.psum_scatter(local_hist, "model", scatter_dimension=1, tiled=True)
        logits = jnp.dot(queries, w_shard, preferred_element_type=jnp.float32)
        lm_max = lax.pmax(jnp.max(logits, axis=1), "model")
        lm_exp = jnp.exp(logits - lm_max[:, None])
        lm_total = lax.psum(jnp.sum(lm_exp, axis=1), "model")
        mix_value = mix_weight[0]
        p_knn = histogram / row_total[:, None]
        p_lm = lm_exp / lm_total[:, None]
        return jnp.log(mix_value * p_knn + (1.0 - mix_value) * p_lm)

    return jax.shard_map(
        local_step,
        mesh=mesh,
        in_specs=(P("data", None), P(None, "model"), P("model", None), P("model"), P(), P()),
        out_specs=P("data", "model"),
        check_vma=False,
    )
```

profile of v0, /device:TPU:112, one launch (start us, length us, event | category | flops | bytes accessed | tf_op | source)
XLA Modules:
  0.0 889.2 jit_solution(1882531150358009653)
XLA Ops:
  6.5 0.0 copy-start
  6.6 0.0 reduce-scatter.2.cloned.1.call-start
  6.6 0.0 copy-start.3
  6.6 40.9 %multiply_reduce_fusion = f32[65536]{0:T(1024)S(1)} fusion(bf16[65536,1024]{1,0:T(8,128)(2,1)} %param.8), kind=kLoop, calls=%fused_computation.1 | loop fusion | flops 201261056 | bytes 134479872 | tf_op jit(solution)/shard_map/reduce_sum | solution.py:14
  48.8 0.0 copy-done
  48.8 0.8 copy-done.3
  49.7 6.0 fusion.8
  55.6 73.7 %fusion.7 = (f32[256]{0:T(256)S(1)}, f32[256,65536]{1,0:T(8,128)}) fusion(f32[]{:T(128)} %bitcast.8, f32[65536]{0:T(1024)S(1)} %multiply_reduce_fusion, bf16[256,1024]{1,0:T(8,128)(2,1)S(1)} %copy-done, bf16[65536,1024]{1,0:T(8,128)(2,1)} %param.8), kind=kOutput, calls=%fused_computation.14 | convolution fusion | flops 34426847232 | bytes 202114048 | tf_op jit(solution)/shard_map/bd,nd->bn/dot_general | solution.py:13
  129.3 16.0 %all-reduce.1 = (f32[256]{0:T(256)S(1)}, f32[256]{0:T(256)S(1)}) all-reduce(f32[256]{0:T(256)S(1)} %get-tuple-element.11, f32[256]{0:T(256)S(1)} %get-tuple-element.13), channel_id=1, replica_groups=mesh['data'=2,'model'=8] {'model'}, use_global_device_ids=true, to_apply=%region_2.0 | all-reduce | flops 512 | bytes 4096 | tf_op jit(solution)/shard_map/pmax | solution.py:16
  145.3 43.0 %fusion.2 = (f32[256]{0:T(256)S(1)}, f32[65536,256]{0,1:T(8,128)}) fusion(f32[256,65536]{1,0:T(8,128)} %get-tuple-element.12, f32[256]{0:T(256)S(1)} %get-tuple-element.7), kind=kLoop, calls=%fused_computation.6 | loop fusion | flops 33554176 | bytes 134219776 | tf_op jit(solution)/shard_map/reduce_sum | solution.py:18
  188.3 0.0 copy-start.2
  188.3 65.9 %copy.7 = f32[65536,256]{1,0:T(8,128)} copy(f32[65536,256]{0,1:T(8,128)} %get-tuple-element.10) | data formatting | bytes 134217728 | tf_op jit(solution)/shard_map/exp | solution.py:17
  254.2 0.0 copy-done.2
  254.2 0.0 copy-start.1
  254.2 369.4 %scatter_custom_fusion = f32[256,50304]{0,1:T(8,128)} fusion(s32[65536]{0:T(1024)S(1)} %compare_select_fusion, f32[65536,256]{1,0:T(8,128)} %copy.7, f32[]{:T(128)} %constant.6.clone.1), kind=kCustom, calls=%fused_computation.8 | custom fusion | flops 16777216 | bytes 51511808 | tf_op jit(solution)/shard_map/scatter-add | solution.py:19
  623.6 0.1 reduce-scatter.2.cloned.1.call-update
  624.3 3.7 fusion.6
  628.1 12.7 %all-reduce = (f32[256]{0:T(256)S(1)}, f32[256]{0:T(256)S(1)}) all-reduce(f32[256]{0:T(256)S(1)} %fusion.6, f32[256]{0:T(256)S(1)} %get-tuple-element.9), channel_id=1, replica_groups=mesh['data'=2,'model'=8] {'model'}, use_global_device_ids=true, to_apply=%region_10.0 | all-reduce | flops 512 | bytes 4096 | tf_op jit(solution)/shard_map/psum | solution.py:24
  640.7 234.1 %reduce-scatter.2.cloned.1.call-done = f32[256,6288]{0,1:T(8,128)} async-done(((f32[256,50304]{0,1:T(8,128)}), f32[256,6288]{0,1:T(8,128)}) %reduce-scatter.2.cloned.1.call-update) | async-done | bytes 6438928 | tf_op jit(solution)/shard_map/reduce_scatter | solution.py:20
  874.8 7.5 add_log_fusion
  882.3 0.0 copy-done.1
  (1 shorter events, 0.0 us)
Async XLA Ops:
  6.5 42.3 %copy-start = (bf16[256,1024]{1,0:T(8,128)(2,1)S(1)}, bf16[256,1024]{1,0:T(8,128)(2,1)}, u32[]{:S(2)}) copy-start(bf16[256,1024]{1,0:T(8,128)(2,1)} %param.6) | copy-start | bytes 1572868
  6.6 868.3 %reduce-scatter.2.cloned.1.call-start = ((), (), s32[]{:S(2)}) async-start(), calls=%async_computation.1 | async-start | bytes 57950208 | tf_op jit(solution)/shard_map/reduce_scatter | solution.py:20
  6.6 43.1 %copy-start.3 = (bf16[1024,6288]{0,1:T(8,128)(2,1)S(1)}, bf16[1024,6288]{0,1:T(8,128)(2,1)}, u32[]{:S(2)}) copy-start(bf16[1024,6288]{0,1:T(8,128)(2,1)} %param.7) | copy-start | bytes 38633476
  188.3 65.9 %copy-start.2 = (s32[65536]{0:T(1024)S(1)}, s32[65536]{0:T(1024)}, u32[]{:S(2)}) copy-start(s32[65536]{0:T(1024)} %param.9) | copy-start | bytes 786436
  254.2 628.1 %copy-start.1 = (bf16[256,1024]{1,0:T(8,128)(2,1)S(1)}, bf16[256,1024]{1,0:T(8,128)(2,1)}, u32[]{:S(2)}) copy-start(bf16[256,1024]{1,0:T(8,128)(2,1)} %param.6) | copy-start | bytes 1572868
Sparse Core Ops, SparseCore 0:
  623.8 250.9 reduce-scatter.1
where the time goes:
time: 890 us; the launch traced here: 889 us
  other arithmetic  465 us (52%)
  waiting for transfers between devices  234 us (26%)
  matrix products  79.7 us (9%)
  local copies, waits for them, and re-layouts  66.7 us (7%)
  blocking collectives  28.7 us (3%)
  between operations  15.5 us (2%)
    scatter-add x1, other arithmetic, local_step(): jnp.zeros((row_count, vocab_size), jnp.float32).at[:, tok_shard]  369 us
    reduce_scatter x1, waiting for transfers between devices, local_step(): lax.psum_scatter(local_hist, 'model', scatter_dimension=1, tiled=True)  234 us
    dot_general x1, matrix products, local_step(): jnp.einsum('bd,nd->bn', queries, key_shard, preferred_element_type=jnp.fl...  73.7 us
    exp x1, local copies, waits for them, and re-layouts, local_step(): weights = jnp.exp(scores - row_max[:, None])  65.9 us
    reduce_sum x1, other arithmetic, local_step(): row_total = lax.psum(jnp.sum(weights, axis=1), 'model')  43 us
    reduce_sum x1, other arithmetic, local_step(): key_sq = jnp.sum(jnp.square(key_shard.astype(jnp.float32)), axis=1)  40.9 us
  transfers between devices with their start and end apart: 1, of which 1 were waited for; matrix products, arithmetic and copies ran while one was open for 0% of the time, Pallas kernels for 0%

commit v1 on v0

v1 whole, which is shorter than its diff:
```python
import functools

import jax
import jax.numpy as jnp
from jax import lax
from jax.experimental import pallas as pl
from jax.experimental.pallas import tpu as pltpu
from jax.sharding import PartitionSpec as P

BLOCK = 1024
UNROLL = 16
GROUPS = 4
SLOTS = 3
SLACK = 40.0


def hist_kernel(inv_tau_ref, flag_ref, tok_ref, keys_ref, qt_ref, out_ref, stat_ref,
                hist, w, sbuf, held, m_ref, z_ref, sems, key_sem):
    i = pl.program_id(0)
    blk = held.shape[1]
    blocks = pl.num_programs(0)

    def fetch(b):
        return pltpu.make_async_copy(keys_ref.at[pl.ds(b * blk, blk), :], held.at[b % SLOTS], key_sem.at[b % SLOTS])

    @pl.when(i == 0)
    def _():
        for b in range(SLOTS - 1):
            fetch(b).start()

    @pl.when(i + SLOTS - 1 < blocks)
    def _():
        fetch(i + SLOTS - 1).start()
    fetch(i).wait()
    key_ref = held.at[i % SLOTS]
    stride = blk // UNROLL
    total = hist.shape[0]
    H = lambda t: pl.ds(pl.multiple_of(t, 2), 2)
    W = lambda e: pl.ds(pl.multiple_of(2 * e, 2), 2)

    inv_tau = inv_tau_ref[0]
    qt = qt_ref[...]
    mb = None
    for r in range(0, blk, 256):
        k = key_ref[pl.ds(r, 256), :]
        c = jnp.dot(k, qt, preferred_element_type=jnp.float32)
        kf = k.astype(jnp.float32)
        sq = jnp.sum(kf * kf, axis=1, keepdims=True)
        s = (2.0 * c - sq) * inv_tau
        sbuf[pl.ds(r, 256), :] = s
        mx = jnp.max(s, axis=0, keepdims=True)
        mb = mx if mb is None else jnp.maximum(mb, mx)
    mb2 = jnp.concatenate([mb[:, :128], mb[:, 128:]], axis=0)

    @pl.when(i == 0)
    def _():
        m_ref[...] = mb2
        z_ref[...] = jnp.zeros_like(z_ref)

        def zero(t, c):
            hist[pl.ds(pl.multiple_of(t * 96, 96), 96), :] = jnp.zeros((96, 128), jnp.float32)
            return c
        lax.fori_loop(0, total // 96, zero, 0)

    @pl.when(jnp.max(mb2 - m_ref[...]) > SLACK)
    def _():
        new = jnp.maximum(m_ref[...], mb2)
        f = jnp.exp(m_ref[...] - new)
        m_ref[...] = new
        z_ref[...] = z_ref[...] * f
        f96 = jnp.concatenate([f] * 48, axis=0)

        def scale(t, c):
            sl = pl.ds(pl.multiple_of(t * 96, 96), 96)
            hist[sl, :] = hist[sl, :] * f96
            return c
        lax.fori_loop(0, total // 96, scale, 0)

    m = m_ref[...]
    mrow = jnp.concatenate([m[0:1], m[1:2]], axis=1)

    def expo(t, acc):
        e = jnp.exp(sbuf[pl.ds(pl.multiple_of(t * 64, 64), 64), :] - mrow)
        w[pl.ds(pl.multiple_of(t * 128, 128), 64, stride=2), :] = e[:, :128]
        w[pl.ds(pl.multiple_of(t * 128, 128) + 1, 64, stride=2), :] = e[:, 128:]
        return acc + jnp.sum(e.reshape(8, 8, 256), axis=0)
    za = lax.fori_loop(0, blk // 64, expo, jnp.zeros((8, 256), jnp.float32))
    za = jnp.sum(za, axis=0, keepdims=True)
    z_ref[...] = z_ref[...] + jnp.concatenate([za[:, :128], za[:, 128:]], axis=0)

    def step(g, c):
        def fast():
            for gg in range(GROUPS):
                at = [g * GROUPS + gg + u * stride for u in range(UNROLL)]
                ts = [tok_ref[0, 0, a] for a in at]
                vs = [hist[H(t), :] + w[W(a), :] for t, a in zip(ts, at)]
                for t, v in zip(ts, vs):
                    hist[H(t), :] = v

        def slow():
            def one(e, c):
                a = g * GROUPS + e // UNROLL + (e % UNROLL) * stride
                t = tok_ref[0, 0, a]
                hist[H(t), :] = hist[H(t), :] + w[W(a), :]
                return c
            lax.fori_loop(0, GROUPS * UNROLL, one, 0)
        lax.cond(flag_ref[0, 0, g] == 0, fast, slow)
        return c
    lax.fori_loop(0, stride // GROUPS, step, 0)

    @pl.when(i == pl.num_programs(0) - 1)
    def _():
        stat_ref[0:2, :] = m_ref[...]
        stat_ref[2:4, :] = z_ref[...]
        stat_ref[4:8, :] = jnp.zeros((4, 128), jnp.float32)
        part = total // 8
        copies = [pltpu.make_async_copy(hist.at[pl.ds(p * part, part), :], out_ref.at[pl.ds(p * part, part), :], sems.at[p])
                  for p in range(8)]
        for copy in copies:
            copy.start()
        for copy in copies:
            copy.wait()


def histogram(keys, qt, tok, inv_tau, vocab):
    count, depth = keys.shape
    blocks = count // BLOCK
    stride = BLOCK // UNROLL
    members = tok.reshape(blocks, UNROLL, stride)
    clash = jnp.zeros((blocks, stride), jnp.bool_)
    for d in range(1, UNROLL):
        clash = clash | jnp.any(members[:, d:] == members[:, :-d], axis=1)
    flags = jnp.any(clash.reshape(blocks, 1, stride // GROUPS, GROUPS), axis=3).astype(jnp.int32)
    f32 = jnp.float32
    return pl.pallas_call(
        hist_kernel,
        grid=(blocks,),
        out_shape=(jax.ShapeDtypeStruct((2 * vocab, 128), f32), jax.ShapeDtypeStruct((8, 128), f32)),
        in_specs=[
            pl.BlockSpec(memory_space=pltpu.SMEM),
            pl.BlockSpec((1, 1, stride // GROUPS), lambda i: (i, 0, 0), memory_space=pltpu.SMEM),
            pl.BlockSpec((1, 1, BLOCK), lambda i: (i, 0, 0), memory_space=pltpu.SMEM),
            pl.BlockSpec(memory_space=pl.ANY),
            pl.BlockSpec((depth, qt.shape[1]), lambda i: (0, 0)),
        ],
        out_specs=(pl.BlockSpec(memory_space=pl.ANY), pl.BlockSpec((8, 128), lambda i: (0, 0))),
        scratch_shapes=[
            pltpu.VMEM((2 * vocab, 128), f32),
            pltpu.VMEM((2 * BLOCK, 128), f32),
            pltpu.VMEM((BLOCK, qt.shape[1]), f32),
            pltpu.VMEM((SLOTS, BLOCK, depth), keys.dtype),
            pltpu.VMEM((2, 128), f32),
            pltpu.VMEM((2, 128), f32),
            pltpu.SemaphoreType.DMA((8,)),
            pltpu.SemaphoreType.DMA((SLOTS,)),
        ],
        compiler_params=pltpu.CompilerParams(vmem_limit_bytes=67043328, dimension_semantics=("arbitrary",)),
        name="histogram",
    )(inv_tau, flags, (2 * tok).reshape(blocks, 1, BLOCK), keys, qt)


def exchange_kernel(group, mix_ref, stat_ref, qt_ref, hist_ref, wt_ref, out_ref,
                    sib, fwd, fin, own, lm, wtile, obuf, stats, lmstat, lmstats,
                    sib_send, sib_recv, fwd_send, fwd_recv, fin_send, fin_recv,
                    st_send, st_recv, ls_send, ls_recv, own_sem, w_sem, o_sem):
    chips = group // 2
    me = lax.axis_index("model")
    x, core = me // 2, me % 2
    sibling = 2 * x + 1 - core
    right = 2 * ((x + 1) % chips) + core
    left = 2 * ((x + chips - 1) % chips) + core
    side = (right, left)
    subs = fwd.shape[1]
    rows = fwd.shape[2]
    toks = rows // 2
    half_rows = subs * rows
    block_rows = 2 * half_rows
    where = lambda d: dict(device_id={"model": d}, device_id_type=pl.DeviceIdType.MESH)

    def place(stage, s, d, c):
        chip = {0: (x + 2) % chips, 1: (x + (1, chips - 1)[d]) % chips, 2: (x + (1, chips - 1)[d]) % chips, 3: x}[stage]
        half = 1 - d if stage == 1 else d
        return pl.ds(pl.multiple_of((2 * chip + c) * block_rows + half * half_rows + s * rows, 8), rows)

    def order(stage, s, d):
        return (stage * subs + s) * 2 + d

    def to_sibling(stage, s, d):
        k = order(stage, s, d)
        return pltpu.make_async_remote_copy(hist_ref.at[place(stage, s, d, 1 - core), :], sib.at[k],
                                            sib_send.at[k], sib_recv.at[k], **where(sibling))

    def own_copy(stage, s, d):
        return pltpu.make_async_copy(hist_ref.at[place(stage, s, d, core), :], own.at[d], own_sem.at[d])

    def hop(d, s):
        return pltpu.make_async_remote_copy(sib.at[order(0, s, d)], fwd.at[d, s], fwd_send.at[d, s], fwd_recv.at[d, s], **where(side[d]))

    def last(d, stage, s):
        k = (stage - 1) * subs + s
        return pltpu.make_async_remote_copy(sib.at[order(stage, s, d)], fin.at[d, k], fin_send.at[d, k], fin_recv.at[d, k], **where(side[d]))

    barrier = pltpu.get_barrier_semaphore()
    for j in range(1, group):
        pl.semaphore_signal(barrier, inc=1, **where((me + j) % group))
    pl.semaphore_wait(barrier, group - 1)

    def stat_copy(j):
        return pltpu.make_async_remote_copy(stat_ref, stats.at[me], st_send.at[j], st_recv.at[j], **where((me + j) % group))

    for j in range(1, group):
        stat_copy(j).start()
    for stage in range(4):
        def issue(s, c, stage=stage):
            for d in range(2):
                to_sibling(stage, s, d).start()
            return c
        lax.fori_loop(0, subs, issue, 0)
    own_copy(0, 0, 0).start()
    own_copy(0, 0, 1).start()
    stats[me] = stat_ref[...]
    tiles = lm.shape[0] // toks

    def w_copy(t):
        return pltpu.make_async_copy(wt_ref.at[pl.ds(t * toks, toks), :], wtile, w_sem)
    w_copy(0).start()
    for j in range(1, group):
        stat_copy(j).wait()

    ms = [stats[i, 0:2, :] for i in range(group)]
    top = functools.reduce(jnp.maximum, ms)
    total = functools.reduce(jnp.add, [stats[i, 2:4, :] * jnp.exp(ms[i] - top) for i in range(group)])
    tile8 = lambda v: jnp.concatenate([v] * 4, axis=0)[None]
    mine = tile8(jnp.exp(stats[me, 0:2, :] - top))
    other = tile8(jnp.exp(stats[sibling, 0:2, :] - top))
    fold = lambda v: v.reshape(rows // 8, 8, 128)

    def merge(stage, s, d):
        k = order(stage, s, d)
        own_copy(stage, s, d).wait()
        to_sibling(stage, s, d).wait_recv()
        return fold(own[d]) * mine + fold(sib[k]) * other

    def prefetch(stage, s, d):
        @pl.when(s + 1 < subs)
        def _():
            own_copy(stage, s + 1, d).start()
        if stage < 3:
            @pl.when(s + 1 == subs)
            def _():
                own_copy(stage + 1, 0, d).start()

    def stage0(s, c):
        for d in range(2):
            v = merge(0, s, d)
            sib[order(0, s, d)] = v.reshape(rows, 128)
            hop(d, s).start()
            prefetch(0, s, d)
        return c
    lax.fori_loop(0, subs, stage0, 0)

    def stage1(s, c):
        for d in range(2):
            v = merge(1, s, d)
            sib[order(1, s, d)] = v.reshape(rows, 128)
            last(d, 1, s).start()
            prefetch(1, s, d)
        return c
    lax.fori_loop(0, subs, stage1, 0)

    qt = qt_ref[...]
    peak = None
    for t in range(tiles):
        w_copy(t).wait()
        logits = jnp.dot(wtile[...], qt, preferred_element_type=jnp.float32)
        lm[pl.ds(t * toks, toks), :] = logits
        if t + 1 < tiles:
            w_copy(t + 1).start()
        mx = jnp.max(logits.reshape(toks // 8, 8, 256), axis=0)
        peak = mx if peak is None else jnp.maximum(peak, mx)
    peak = jnp.max(peak, axis=0, keepdims=True)

    def expo(t, acc):
        sl = pl.ds(pl.multiple_of(t * 48, 48), 48)
        e = jnp.exp(lm[sl, :] - peak)
        lm[sl, :] = e
        return acc + jnp.sum(e.reshape(6, 8, 256), axis=0)
    acc = lax.fori_loop(0, lm.shape[0] // 48, expo, jnp.zeros((8, 256), jnp.float32))
    acc = jnp.sum(acc, axis=0, keepdims=True)
    lmstat[0:1, :] = peak
    lmstat[1:2, :] = acc
    lmstat[2:8, :] = jnp.zeros((6, 256), jnp.float32)
    lmstats[me, 0:1, :] = peak
    lmstats[me, 1:2, :] = acc

    def ls_copy(j):
        return pltpu.make_async_remote_copy(lmstat, lmstats.at[me], ls_send.at[j], ls_recv.at[j], **where((me + j) % group))

    def stage2(s, c):
        for d in range(2):
            v = merge(2, s, d)
            hop(d, s).wait_recv()
            sib[order(2, s, d)] = (v + fold(fwd[d, s])).reshape(rows, 128)
            last(d, 2, s).start()
            prefetch(2, s, d)
        return c

    for j in range(1, group):
        ls_copy(j).start()
    lax.fori_loop(0, subs, stage2, 0)
    for j in range(1, group):
        ls_copy(j).wait()

    lms = [lmstats[i, 0:1, :] for i in range(group)]
    lm_top = functools.reduce(jnp.maximum, lms)
    lm_total = functools.reduce(jnp.add, [lmstats[i, 1:2, :] * jnp.exp(lms[i] - lm_top) for i in range(group)])
    mix = mix_ref[0]
    lm_scale = (1.0 - mix) * (jnp.exp(peak - lm_top) / lm_total)
    knn_scale = mix / total
    knn_row = jnp.concatenate([knn_scale[0:1], knn_scale[1:2]], axis=1)

    def out_copy(s, d):
        return pltpu.make_async_copy(obuf.at[d], out_ref.at[pl.ds(pl.multiple_of((d * subs + s) * toks, 8), toks), :], o_sem.at[d])

    def stage3(s, c):
        for d in range(2):
            k = order(3, s, d)
            v = merge(3, s, d)
            last(1 - d, 1, s).wait_recv()
            v = v + fold(fin[1 - d, s])
            last(d, 2, s).wait_recv()
            v = v + fold(fin[d, subs + s])
            sib[k] = v.reshape(rows, 128)
            prefetch(3, s, d)

            @pl.when(s > 0)
            def _():
                out_copy(s - 1, d).wait()
            hk = jnp.concatenate([sib[k, pl.ds(0, toks, stride=2), :], sib[k, pl.ds(1, toks, stride=2), :]], axis=1)
            e = lm[pl.ds(pl.multiple_of((d * subs + s) * toks, 8), toks), :]
            obuf[d] = hk * knn_row + e * lm_scale
            out_copy(s, d).start()
        return c
    lax.fori_loop(0, subs, stage3, 0)
    for d in range(2):
        out_copy(subs - 1, d).wait()

    def drain(s, c):
        for stage in range(4):
            for d in range(2):
                to_sibling(stage, s, d).wait_send()
        for d in range(2):
            hop(d, s).wait_send()
            last(d, 1, s).wait_send()
            last(d, 2, s).wait_send()
        return c
    lax.fori_loop(0, subs, drain, 0)


def exchange(hist, stat, qt, wt, mix, group):
    cols = wt.shape[0]
    subs = next(n for n in range(3, cols) if cols % (2 * n * 8) == 0)
    toks = cols // (2 * subs)
    rows = 2 * toks
    dma = pltpu.SemaphoreType.DMA
    f32 = jnp.float32
    return pl.pallas_call(
        functools.partial(exchange_kernel, group),
        out_shape=jax.ShapeDtypeStruct((cols, qt.shape[1]), f32),
        in_specs=[
            pl.BlockSpec(memory_space=pltpu.SMEM),
            pl.BlockSpec(memory_space=pltpu.VMEM),
            pl.BlockSpec(memory_space=pltpu.VMEM),
            pl.BlockSpec(memory_space=pl.ANY),
            pl.BlockSpec(memory_space=pl.ANY),
        ],
        out_specs=pl.BlockSpec(memory_space=pl.ANY),
        scratch_shapes=[
            pltpu.VMEM((8 * subs, rows, 128), f32),
            pltpu.VMEM((2, subs, rows, 128), f32),
            pltpu.VMEM((2, 2 * subs, rows, 128), f32),
            pltpu.VMEM((2, rows, 128), f32),
            pltpu.VMEM((cols, qt.shape[1]), f32),
            pltpu.VMEM((toks, wt.shape[1]), wt.dtype),
            pltpu.VMEM((2, toks, qt.shape[1]), f32),
            pltpu.VMEM((group, 8, 128), f32),
            pltpu.VMEM((8, qt.shape[1]), f32),
            pltpu.VMEM((group, 8, qt.shape[1]), f32),
            dma((8 * subs,)), dma((8 * subs,)),
            dma((2, subs)), dma((2, subs)),
            dma((2, 2 * subs)), dma((2, 2 * subs)),
            dma((group,)), dma((group,)), dma((group,)), dma((group,)),
            dma((2,)), dma, dma((2,)),
        ],
        compiler_params=pltpu.CompilerParams(collective_id=0, has_side_effects=True, vmem_limit_bytes=67043328),
        name="exchange",
    )(mix, stat, qt, hist, wt)


def solution(mesh):
    group = mesh.shape["model"]

    def local_step(queries, w_shard, key_shard, tok_shard, temperature, mix_weight):
        qt = queries.T
        vocab = w_shard.shape[1] * group
        hist, stat = histogram(key_shard, qt, tok_shard, 1.0 / temperature, vocab)
        mixed = exchange(hist, stat, qt, w_shard.T, mix_weight, group)
        return jnp.log(mixed).T

    return jax.shard_map(
        local_step,
        mesh=mesh,
        in_specs=(P("data", None), P(None, "model"), P("model", None), P("model"), P(), P()),
        out_specs=P("data", "model"),
        check_vma=False,
    )
```

time: 890 us -> 475 us (0.53)
  other arithmetic: 465 us -> 4.57 us
  Pallas kernels: 0 us -> 460 us
  waiting for transfers between devices: 234 us -> 0 us
  matrix products: 79.7 us -> 0 us
  local copies, waits for them, and re-layouts: 66.7 us -> 8.82 us
  blocking collectives: 28.7 us -> 0 us
  between operations: 15.5 us -> 1.46 us
    pallas_call x0 -> x2, Pallas kernels: none -> 460 us  [the longest x1 236 us: histogram(): pl.pallas_call(hist_kernel, grid=(blocks,), out_shape=(jax.ShapeDtypeStru...]
    scatter-add x1 -> x0, other arithmetic: 369 us -> none  [local_step(): jnp.zeros((row_count, vocab_size), jnp.float32).at[:, tok_shard]]
    reduce_scatter x1 -> x0, waiting for transfers between devices: 234 us -> none  [local_step(): lax.psum_scatter(local_hist, 'model', scatter_dimension=1, tiled=True)]
    reduce_sum x3 -> x0, other arithmetic: 87.6 us -> none  [the longest x1 43 us: local_step(): row_total = lax.psum(jnp.sum(weights, axis=1), 'model')]
    dot_general x2 -> x0, matrix products: 79.7 us -> none  [the longest x1 73.7 us: local_step(): jnp.einsum('bd,nd->bn', queries, key_shard, preferred_element_type=jnp.fl...]
    exp x1 -> x0, local copies, waits for them, and re-layouts: 65.9 us -> none  [local_step(): weights = jnp.exp(scores - row_max[:, None])]
    pmax x1 -> x0, blocking collectives: 16 us -> none  [local_step(): row_max = lax.pmax(jnp.max(scores, axis=1), 'model')]
    psum x1 -> x0, blocking collectives: 12.7 us -> none  [local_step(): lm_total = lax.psum(jnp.sum(lm_exp, axis=1), 'model')]
  transfers between devices with their start and end apart: 1 -> 0, of which waited for: 1 -> 0; matrix products, arithmetic and copies ran while one was open for 0% -> 0% of each run, Pallas kernels for 0% -> 0%
where the time goes in v1:
time: 475 us
  Pallas kernels  460 us (97%)
  local copies, waits for them, and re-layouts  8.82 us (2%)
    pallas_call x1, Pallas kernels, histogram(): pl.pallas_call(hist_kernel, grid=(blocks,), out_shape=(jax.ShapeDtypeStru...  236 us
    pallas_call x1, Pallas kernels, exchange(): pl.pallas_call(functools.partial(exchange_kernel, group), out_shape=jax.S...  224 us

profile of v1, /device:TPU:112, one launch (start us, length us, event | category | flops | bytes accessed | tf_op | source)
XLA Modules:
  0.0 474.7 jit_solution(13456795067140868932)
XLA Ops:
  0.0 0.0 copy-start
  1.4 1.7 broadcast_multiply_fusion
  3.1 1.1 reshape.212
  4.2 0.1 fusion.9
  4.3 0.2 fusion.6
  4.5 0.2 fusion.5
  4.7 0.1 fusion.7
  4.8 0.2 fusion.4
  5.0 0.1 compare_reduce_fusion
  5.1 0.2 fusion.3
  5.3 0.1 fusion.8
  5.4 0.2 fusion.2
  5.6 0.1 fusion.12
  5.7 0.2 fusion.1
  5.9 0.1 fusion.10
  6.0 0.2 fusion
  6.2 0.1 fusion.11
  6.3 0.1 slice_compare_fusion.13
  6.4 0.1 copy.12
  6.5 0.1 copy.11
  6.7 0.1 copy.13
  6.8 0.6 convert_element_type.7
  7.4 0.0 copy-done
  7.4 1.0 copy.14
  8.4 235.8 %histogram.1 = (f32[100608,128]{1,0:T(8,128)}, f32[8,128]{1,0:T(8,128)}) custom-call(f32[1]{0:T(128)S(6)} %div.3.inv_tau_ref, s32[64,1,16]{2,1,0:T(1,128)} %bitcast.12, s32[64,1,1024]{2,1,0:T(1,128)} %bitcast.11, bf16[65536,1024]{1,0:T(8,128)(2,1)} %keys_ref.1, bf16[1024,256]{1,0:T(8,128)(2,1)} %bitcast.9), custom_call_target="tpu_custom_call" | custom-call | tf_op jit(solution)/shard_map/histogram/pallas_call | solution.py:135
  244.2 224.0 %exchange.1 = f32[6288,256]{1,0:T(8,128)} custom-call(f32[1]{0:T(128)S(6)} %copy.16.mix_ref, f32[8,128]{1,0:T(8,128)} %get-tuple-element.7.stat_ref, bf16[1024,256]{1,0:T(8,128)(2,1)} %bitcast.10, f32[100608,128]{1,0:T(8,128)} %get-tuple-element.8.hist_ref, bf16[6288,1024]{1,0:T(8,128)(2,1)} %bitcast.8), custom_call_target="tpu_custom_call" | custom-call | tf_op jit(solution)/shard_map/exchange/pallas_call | solution.py:367
  468.2 6.4 %log_bitcast_fusion = f32[256,6288]{0,1:T(8,128)} fusion(f32[6288,256]{1,0:T(8,128)} %exchange.1), kind=kLoop, calls=%fused_computation | loop fusion | bytes 12877824 | tf_op jit(solution)/shard_map/transpose | solution.py:408
  (2 shorter events, 0.1 us)
Async XLA Ops:
  0.0 7.4 %copy-start = (bf16[256,1024]{1,0:T(8,128)(2,1)S(1)}, bf16[256,1024]{1,0:T(8,128)(2,1)}, u32[]{:S(2)}) copy-start(bf16[256,1024]{1,0:T(8,128)(2,1)} %param.6) | copy-start | bytes 1572868

commit v2 on v1

--- a/solution.py
+++ b/solution.py
@@ -7,156 +7,217 @@
 from jax.experimental.pallas import tpu as pltpu
 from jax.sharding import PartitionSpec as P
 
-BLOCK = 1024
-UNROLL = 16
-GROUPS = 4
-SLOTS = 3
+CHUNK = 512
+PIECE = 256
+UNROLL = 4
+SLOTS = 5
 SLACK = 40.0
-
-
-def hist_kernel(inv_tau_ref, flag_ref, tok_ref, keys_ref, qt_ref, out_ref, stat_ref,
-                hist, w, sbuf, held, m_ref, z_ref, sems, key_sem):
-    i = pl.program_id(0)
-    blk = held.shape[1]
-    blocks = pl.num_programs(0)
-
-    def fetch(b):
-        return pltpu.make_async_copy(keys_ref.at[pl.ds(b * blk, blk), :], held.at[b % SLOTS], key_sem.at[b % SLOTS])
-
-    @pl.when(i == 0)
-    def _():
-        for b in range(SLOTS - 1):
-            fetch(b).start()
-
-    @pl.when(i + SLOTS - 1 < blocks)
-    def _():
-        fetch(i + SLOTS - 1).start()
-    fetch(i).wait()
-    key_ref = held.at[i % SLOTS]
-    stride = blk // UNROLL
-    total = hist.shape[0]
+STEP = 32
+
+
+def hist_kernel(inv_tau_ref, zero_ref, first_ref, next_ref, used_ref, rows_ref, keys_ref, qt_ref, out_ref, stat_ref,
+                hist, w_a, w_b, held, t_a, t_b, t_c, t_d, all_ref, m_ref, peak_ref, part_ref, z_ref, sems, key_sem, tok_sem):
+    size = held.shape[1]
+    chunks = keys_ref.shape[0] // size
+    stride = size // UNROLL
+    total = out_ref.shape[0]
+    zero = zero_ref[0]
     H = lambda t: pl.ds(pl.multiple_of(t, 2), 2)
-    W = lambda e: pl.ds(pl.multiple_of(2 * e, 2), 2)
-
-    inv_tau = inv_tau_ref[0]
-    qt = qt_ref[...]
-    mb = None
-    for r in range(0, blk, 256):
-        k = key_ref[pl.ds(r, 256), :]
-        c = jnp.dot(k, qt, preferred_element_type=jnp.float32)
-        kf = k.astype(jnp.float32)
-        sq = jnp.sum(kf * kf, axis=1, keepdims=True)
-        s = (2.0 * c - sq) * inv_tau
-        sbuf[pl.ds(r, 256), :] = s
-        mx = jnp.max(s, axis=0, keepdims=True)
-        mb = mx if mb is None else jnp.maximum(mb, mx)
-    mb2 = jnp.concatenate([mb[:, :128], mb[:, 128:]], axis=0)
-
-    @pl.when(i == 0)
-    def _():
-        m_ref[...] = mb2
-        z_ref[...] = jnp.zeros_like(z_ref)
-
-        def zero(t, c):
-            hist[pl.ds(pl.multiple_of(t * 96, 96), 96), :] = jnp.zeros((96, 128), jnp.float32)
-            return c
-        lax.fori_loop(0, total // 96, zero, 0)
-
-    @pl.when(jnp.max(mb2 - m_ref[...]) > SLACK)
-    def _():
-        new = jnp.maximum(m_ref[...], mb2)
-        f = jnp.exp(m_ref[...] - new)
-        m_ref[...] = new
-        z_ref[...] = z_ref[...] * f
-        f96 = jnp.concatenate([f] * 48, axis=0)
-
-        def scale(t, c):
-            sl = pl.ds(pl.multiple_of(t * 96, 96), 96)
-            hist[sl, :] = hist[sl, :] * f96
-            return c
-        lax.fori_loop(0, total // 96, scale, 0)
-
-    m = m_ref[...]
-    mrow = jnp.concatenate([m[0:1], m[1:2]], axis=1)
-
-    def expo(t, acc):
-        e = jnp.exp(sbuf[pl.ds(pl.multiple_of(t * 64, 64), 64), :] - mrow)
-        w[pl.ds(pl.multiple_of(t * 128, 128), 64, stride=2), :] = e[:, :128]
-        w[pl.ds(pl.multiple_of(t * 128, 128) + 1, 64, stride=2), :] = e[:, 128:]
-        return acc + jnp.sum(e.reshape(8, 8, 256), axis=0)
-    za = lax.fori_loop(0, blk // 64, expo, jnp.zeros((8, 256), jnp.float32))
-    za = jnp.sum(za, axis=0, keepdims=True)
-    z_ref[...] = z_ref[...] + jnp.concatenate([za[:, :128], za[:, 128:]], axis=0)
-
-    def step(g, c):
-        def fast():
-            for gg in range(GROUPS):
-                at = [g * GROUPS + gg + u * stride for u in range(UNROLL)]
-                ts = [tok_ref[0, 0, a] for a in at]
-                vs = [hist[H(t), :] + w[W(a), :] for t, a in zip(ts, at)]
-                for t, v in zip(ts, vs):
+    W = lambda e: pl.ds(pl.multiple_of(zero + 2 * e, 2), 2)
+    twice = 2.0 * inv_tau_ref[0]
+
+    def fetch(c):
+        return pltpu.make_async_copy(keys_ref.at[pl.ds(c * size, size), :], held.at[c % SLOTS], key_sem.at[c % SLOTS])
+
+    tokens = (t_a, t_b, t_c, t_d)
+    turns = len(tokens)
+
+    def tok_fetch(c, turn):
+        return [pltpu.make_async_copy(used_ref.at[c], tokens[turn], tok_sem.at[turn, 0]),
+                pltpu.make_async_copy(rows_ref.at[c], all_ref.at[turn], tok_sem.at[turn, 1])]
+
+    def score(c, w, beside=()):
+        slot = c % SLOTS
+        qt = qt_ref[...]
+        m8 = m_ref[...]
+        peak, part = None, None
+        for r in range(0, size, PIECE):
+            cross = jnp.dot(held[slot, pl.ds(r, PIECE), :], qt, preferred_element_type=jnp.float32)
+            for b in range(0, PIECE, STEP):
+                kf = held[slot, pl.ds(r + b, STEP), :].astype(jnp.float32)
+                half = 0.5 * jnp.sum(kf * kf, axis=1, keepdims=True)
+                s = ((cross[b:b + STEP] - half) * twice).reshape(STEP // 8, 8, 256)
+                e = jnp.exp(s - m8[None])
+                mx, sm = jnp.max(s, axis=0), jnp.sum(e, axis=0)
+                peak = mx if peak is None else jnp.maximum(peak, mx)
+                part = sm if part is None else part + sm
+                e = e.reshape(STEP, 256)
+                w[pl.ds(2 * (r + b), STEP, stride=2), :] = e[:, :128]
+                w[pl.ds(2 * (r + b) + 1, STEP, stride=2), :] = e[:, 128:]
+        for add in beside:
+            add()
+        peak_ref[...] = peak
+        part_ref[...] = part
+        return jnp.max(peak - m8) > SLACK
+
+    def spread(v):
+        return jnp.broadcast_to(jnp.max(v, axis=0, keepdims=True), v.shape)
+
+    def adds(turn, w):
+        toks = tokens[turn]
+        ahead = []
+
+        def step(j):
+            if j < stride:
+                ts = [toks[0, j + u * stride] for u in range(UNROLL)]
+                ahead.append([(t, hist[H(t), :] + w[W(j + u * stride), :]) for u, t in enumerate(ts)])
+            if j > 0:
+                for t, v in ahead.pop(0):
                     hist[H(t), :] = v
-
-        def slow():
-            def one(e, c):
-                a = g * GROUPS + e // UNROLL + (e % UNROLL) * stride
-                t = tok_ref[0, 0, a]
-                hist[H(t), :] = hist[H(t), :] + w[W(a), :]
-                return c
-            lax.fori_loop(0, GROUPS * UNROLL, one, 0)
-        lax.cond(flag_ref[0, 0, g] == 0, fast, slow)
-        return c
-    lax.fori_loop(0, stride // GROUPS, step, 0)
-
-    @pl.when(i == pl.num_programs(0) - 1)
-    def _():
-        stat_ref[0:2, :] = m_ref[...]
-        stat_ref[2:4, :] = z_ref[...]
-        stat_ref[4:8, :] = jnp.zeros((4, 128), jnp.float32)
-        part = total // 8
-        copies = [pltpu.make_async_copy(hist.at[pl.ds(p * part, part), :], out_ref.at[pl.ds(p * part, part), :], sems.at[p])
-                  for p in range(8)]
-        for copy in copies:
+        return [functools.partial(step, j) for j in range(stride + 1)]
+
+    def repeats(c, turn, w):
+        def step(j):
+            def one(u, carry):
+                a = j + u * stride
+                t = all_ref[turn, 0, a]
+
+                @pl.when(tokens[turn][0, a] != t)
+                def _():
+                    hist[H(t), :] = hist[H(t), :] + w[W(a), :]
+                return carry
+            lax.fori_loop(0, UNROLL, one, 0)
+            return next_ref[c * stride + j]
+        lax.while_loop(lambda j: j < stride, step, first_ref[c])
+
+    def advance(c, turn, cur, nxt):
+        for copy in tok_fetch(c, turn):
+            copy.wait()
+
+        @pl.when(c + turns - 1 < chunks)
+        def _():
+            for copy in tok_fetch(c + turns - 1, (turn + turns - 1) % turns):
+                copy.start()
+
+        @pl.when(c + 1 < chunks)
+        def _():
+            fetch(c + 1).wait()
+
+        @pl.when(c + SLOTS - 1 < chunks)
+        def _():
+            fetch(c + SLOTS - 1).start()
+
+        over = score(c + 1, nxt, adds(turn, cur))
+
+        repeats(c, turn, cur)
+
+        @pl.when(over & (c + 1 < chunks))
+        def _():
+            old = m_ref[...]
+            new = spread(jnp.maximum(old, peak_ref[...]))
+            f = jnp.exp(old - new)
+            m_ref[...] = new
+            z_ref[...] = z_ref[...] * f
+            pair = jnp.concatenate([f[0:1, :128], f[0:1, 128:]], axis=0)
+            f96 = jnp.concatenate([pair] * 48, axis=0)
+
+            def scale(t, carry):
+                sl = pl.ds(pl.multiple_of(t * 96, 96), 96)
+                hist[sl, :] = hist[sl, :] * f96
+                return carry
+            lax.fori_loop(0, total // 96, scale, 0)
+            score(c + 1, nxt)
+
+        @pl.when(c + 1 < chunks)
+        def _():
+            z_ref[...] = z_ref[...] + part_ref[...]
+
+    for c in range(turns - 1):
+        for copy in tok_fetch(c, c):
             copy.start()
-        for copy in copies:
-            copy.wait()
+    for c in range(SLOTS - 1):
+        fetch(c).start()
+
+    def clear(t, carry):
+        hist[pl.ds(pl.multiple_of(t * 96, 96), 96), :] = jnp.zeros((96, 128), jnp.float32)
+        return carry
+    lax.fori_loop(0, total // 96, clear, 0)
+    fetch(0).wait()
+    m_ref[...] = jnp.zeros_like(m_ref)
+
+    def first(t, carry):
+        score(0, w_a)
+        m_ref[...] = spread(peak_ref[...])
+        return carry
+    lax.fori_loop(0, 2, first, 0)
+    z_ref[...] = part_ref[...]
+
+    def round_of(p, carry):
+        for turn in range(turns):
+            cur, nxt = (w_a, w_b) if turn % 2 == 0 else (w_b, w_a)
+            advance(turns * p + turn, turn, cur, nxt)
+        return carry
+    lax.fori_loop(0, chunks // turns, round_of, 0)
+
+    rows = lambda v: jnp.concatenate([v[:, :128], v[:, 128:]], axis=0)
+    stat_ref[0:2, :] = rows(m_ref[0:1, :])
+    stat_ref[2:4, :] = rows(jnp.sum(z_ref[...], axis=0, keepdims=True))
+    stat_ref[4:8, :] = jnp.zeros((4, 128), jnp.float32)
+    part = total // 8
+    copies = [pltpu.make_async_copy(hist.at[pl.ds(p * part, part), :], out_ref.at[pl.ds(p * part, part), :], sems.at[p])
+              for p in range(8)]
+    for copy in copies:
+        copy.start()
+    for copy in copies:
+        copy.wait()
 
 
 def histogram(keys, qt, tok, inv_tau, vocab):
     count, depth = keys.shape
-    blocks = count // BLOCK
-    stride = BLOCK // UNROLL
-    members = tok.reshape(blocks, UNROLL, stride)
-    clash = jnp.zeros((blocks, stride), jnp.bool_)
-    for d in range(1, UNROLL):
-        clash = clash | jnp.any(members[:, d:] == members[:, :-d], axis=1)
-    flags = jnp.any(clash.reshape(blocks, 1, stride // GROUPS, GROUPS), axis=3).astype(jnp.int32)
+    chunks = count // CHUNK
+    stride = CHUNK // UNROLL
+    members = tok.reshape(chunks, UNROLL, stride)
+    ahead = jnp.concatenate([jnp.full((chunks, UNROLL, 1), -1, tok.dtype), members[:, :, :-1]], axis=2)
+    again = []
+    for u in range(UNROLL):
+        at = members[:, u:u + 1]
+        again.append(functools.reduce(
+            jnp.logical_or, [members[:, o] == at[:, 0] for o in range(u)] + [ahead[:, o] == at[:, 0] for o in range(UNROLL)]))
+    again = jnp.stack(again, axis=1)
+    rows = 2 * members
+    used = jnp.where(again, 2 * vocab, rows)
+    group = jnp.where(jnp.any(again, axis=1), lax.broadcasted_iota(jnp.int32, (chunks, stride), 1), stride)
+    coming = lax.cummin(group, axis=1, reverse=True)
+    follow = jnp.concatenate([coming[:, 1:], jnp.full((chunks, 1), stride, jnp.int32)], axis=1)
     f32 = jnp.float32
     return pl.pallas_call(
         hist_kernel,
-        grid=(blocks,),
         out_shape=(jax.ShapeDtypeStruct((2 * vocab, 128), f32), jax.ShapeDtypeStruct((8, 128), f32)),
-        in_specs=[
-            pl.BlockSpec(memory_space=pltpu.SMEM),
-            pl.BlockSpec((1, 1, stride // GROUPS), lambda i: (i, 0, 0), memory_space=pltpu.SMEM),
-            pl.BlockSpec((1, 1, BLOCK), lambda i: (i, 0, 0), memory_space=pltpu.SMEM),
+        in_specs=[pl.BlockSpec(memory_space=pltpu.SMEM)] * 4 + [
             pl.BlockSpec(memory_space=pl.ANY),
-            pl.BlockSpec((depth, qt.shape[1]), lambda i: (0, 0)),
+            pl.BlockSpec(memory_space=pl.ANY),
+            pl.BlockSpec(memory_space=pl.ANY),
+            pl.BlockSpec(memory_space=pltpu.VMEM),
         ],
-        out_specs=(pl.BlockSpec(memory_space=pl.ANY), pl.BlockSpec((8, 128), lambda i: (0, 0))),
+        out_specs=(pl.BlockSpec(memory_space=pl.ANY), pl.BlockSpec(memory_space=pltpu.VMEM)),
         scratch_shapes=[
-            pltpu.VMEM((2 * vocab, 128), f32),
-            pltpu.VMEM((2 * BLOCK, 128), f32),
-            pltpu.VMEM((BLOCK, qt.shape[1]), f32),
-            pltpu.VMEM((SLOTS, BLOCK, depth), keys.dtype),
-            pltpu.VMEM((2, 128), f32),
-            pltpu.VMEM((2, 128), f32),
+            pltpu.VMEM((2 * vocab + 8, 128), f32),
+            pltpu.VMEM((2 * CHUNK, 128), f32),
+            pltpu.VMEM((2 * CHUNK, 128), f32),
+            pltpu.VMEM((SLOTS, CHUNK, depth), keys.dtype),
+            *[pltpu.SMEM((1, CHUNK), jnp.int32)] * 4,
+            pltpu.SMEM((4, 1, CHUNK), jnp.int32),
+            pltpu.VMEM((8, qt.shape[1]), f32),
+            pltpu.VMEM((8, qt.shape[1]), f32),
+            pltpu.VMEM((8, qt.shape[1]), f32),
+            pltpu.VMEM((8, qt.shape[1]), f32),
             pltpu.SemaphoreType.DMA((8,)),
             pltpu.SemaphoreType.DMA((SLOTS,)),
+            pltpu.SemaphoreType.DMA((4, 2)),
         ],
-        compiler_params=pltpu.CompilerParams(vmem_limit_bytes=67043328, dimension_semantics=("arbitrary",)),
+        compiler_params=pltpu.CompilerParams(vmem_limit_bytes=67043328),
         name="histogram",
-    )(inv_tau, flags, (2 * tok).reshape(blocks, 1, BLOCK), keys, qt)
+    )(inv_tau, jnp.zeros((1,), jnp.int32), coming[:, 0], follow.reshape(-1), used.reshape(chunks, 1, CHUNK), rows.reshape(chunks, 1, CHUNK), keys, qt)
 
 
 def exchange_kernel(group, mix_ref, stat_ref, qt_ref, hist_ref, wt_ref, out_ref,

time: 475 us -> 402 us (0.85)
  Pallas kernels: 460 us -> 378 us
  other arithmetic: 4.57 us -> 11.3 us
    pallas_call x1, Pallas kernels: 236 us -> 156 us  [histogram(): pl.pallas_call(hist_kernel, out_shape=(jax.ShapeDtypeStruct((2 * vocab, 1...]
where the time goes in v2:
time: 402 us
  Pallas kernels  378 us (94%)
  other arithmetic  11.3 us (3%)
  local copies, waits for them, and re-layouts  10.5 us (3%)
    pallas_call x1, Pallas kernels, exchange(): pl.pallas_call(functools.partial(exchange_kernel, group), out_shape=jax.S...  222 us
    pallas_call x1, Pallas kernels, histogram(): pl.pallas_call(hist_kernel, out_shape=(jax.ShapeDtypeStruct((2 * vocab, 1...  156 us

profile of v2, /device:TPU:112, one launch (start us, length us, event | category | flops | bytes accessed | tf_op | source)
XLA Modules:
  0.0 401.5 jit_solution(5962565238413074911)
XLA Ops:
  1.3 1.0 broadcast_multiply_fusion
  2.3 0.0 copy-start
  2.3 6.7 %or_or_fusion = (pred[128,1,128]{2,1,0:T(4,128)(4,1)S(1)}, pred[128,1,128]{2,1,0:T(4,128)(4,1)S(1)}, pred[128,1,128]{2,1,0:T(4,128)(4,1)S(1)}, pred[128,1,128]{2,1,0:T(4,128)(4,1)S(1)}, pred[128,1,128]{2,1,0:T(4,128)(4,1)S(1)}) fusion(s32[128,4,127]{2,1,0:T(4,128)} %bitcast.20, s32[128,4,128]{2,1,0:T(4,128)} %bitcast.19), kind=kLoop, calls=%fused_computation.3 | loop fusion | flops 704512 | bytes 604160 | tf_op jit(solution)/shard_map/reduce_or | solution.py:189
  9.0 0.1 copy.14
  9.1 2.2 reduce_window_min.10
  11.3 0.5 slice_bitcast_fusion.first_ref
  11.9 0.1 copy.20
  12.0 0.6 pad_bitcast_fusion.next_ref
  12.6 0.3 pad_add_fusion
  12.9 0.2 copy.16
  13.1 0.5 copy.17
  13.6 0.0 copy-done
  13.6 1.1 broadcast_select_fusion.used_ref
  14.7 2.0 copy.18
  16.8 156.2 %histogram.2 = (f32[100608,128]{1,0:T(8,128)}, f32[8,128]{1,0:T(8,128)}) custom-call(f32[1]{0:T(128)S(6)} %div.3.inv_tau_ref, s32[1]{0:T(128)} %constant.8.clone.1.zero_ref, s32[128]{0:T(128)} %slice_bitcast_fusion.first_ref, s32[16384]{0:T(1024)} %pad_bitcast_fusion.next_ref, s32[128,1,512]{2,1,0:T(1,128)} %broadcast_select_fusion.used_ref, ...), custom_call_target="tpu_custom_call" | custom-call | tf_op jit(solution)/shard_map/histogram/pallas_call | solution.py:193
  173.0 222.0 %exchange.1 = f32[6288,256]{1,0:T(8,128)} custom-call(f32[1]{0:T(128)S(6)} %copy.23.mix_ref, f32[8,128]{1,0:T(8,128)} %get-tuple-element.7.stat_ref, bf16[1024,256]{1,0:T(8,128)(2,1)} %bitcast.16, f32[100608,128]{1,0:T(8,128)} %get-tuple-element.8.hist_ref, bf16[6288,1024]{1,0:T(8,128)(2,1)} %bitcast.14), custom_call_target="tpu_custom_call" | custom-call | tf_op jit(solution)/shard_map/exchange/pallas_call | solution.py:428
  395.1 6.4 %log_bitcast_fusion = f32[256,6288]{0,1:T(8,128)} fusion(f32[6288,256]{1,0:T(8,128)} %exchange.1), kind=kLoop, calls=%fused_computation | loop fusion | bytes 12877824 | tf_op jit(solution)/shard_map/transpose | solution.py:469
  (2 shorter events, 0.0 us)
Async XLA Ops:
  2.3 11.3 %copy-start = (s32[65536]{0:T(1024)}, s32[65536]{0:T(1024)S(1)}, u32[]{:S(2)}) copy-start(s32[65536]{0:T(1024)S(1)} %broadcast_multiply_fusion) | copy-start | bytes 786436
